TPU v7x, 32 devices: a whole 2x2x4 slice. The times are simulated.
32 devices in a mesh: grp: 2 (over y), sp: 16 (over z, x, core).
Axes of the slice: x: 2, y: 2, z: 4, core: 2. Of those that a mesh axis runs over, the one named last changes fastest.
Arguments:
- alpha: float32 [20, 16, 4096], P('grp', None, 'sp'), may hold values from -6 to 6
- ensemble: bfloat16 [20, 3, 16, 4096], P('grp', None, None, 'sp'), may hold values from -6 to 6
- static_std: float32 [3, 16, 4096], P(None, 'grp', 'sp'), may hold values from 0.2 to 1
- control: float32 [3, 16, 4096], P(None, 'grp', 'sp'), may hold values from -6 to 6
- loc_spectrum: float32 [1024], replicated, may hold values from 0.00024414062 to 0.001953125
- obs_cell: int32 [32768], P(('grp', 'sp')), may hold values from 0 to 65535, as said below
- obs_step: int32 [32768], P(('grp', 'sp')), may hold values from 0 to 2
- innovation: float32 [32768], P(('grp', 'sp')), may hold values from -6 to 6
- obs_weight: float32 [32768], P(('grp', 'sp')), may hold values from 0.5 to 4
Outputs:
- grad_alpha: float32 [20, 16, 4096], P('grp', None, 'sp')
- grad_control: float32 [3, 16, 4096], P(None, 'grp', 'sp')
Inputs may be any that keep to these rules, and one draw needn't show every extreme that they name: `obs_cell`: an entry is row * 4096 + column. Entries 1024 * b to 1024 * (b + 1) - 1 lie in the tile of 8 rows from row 8 * (b // 16) and 256 columns from column 256 * (b % 16).
All inputs are finite; a program needn't handle non-finite values.
Results may differ from a plain program's by a relative error of at most 0.0075.
Values may be sent and summed in bfloat16 or wider, within the bound.
A program may use at most 128 MiB of HBM per device.

v0:
```python
import math
import jax
import jax.numpy as jnp
from jax import lax
from jax.sharding import PartitionSpec as P

NX = 4096
courant = 0.4


def extended(block, sides, width):
    for axis, dim in sides:
        count = lax.axis_size(axis)
        forward = [(i, i + 1) for i in range(count - 1)]
        forward.append((count - 1, 0))
        backward = [(target, source) for source, target in forward]
        low = lax.ppermute(
            lax.slice_in_dim(block, block.shape[dim] - width, None, axis=dim), axis, forward
        )
        high = lax.ppermute(lax.slice_in_dim(block, 0, width, axis=dim), axis, backward)
        block = jnp.concatenate([low, block, high], axis=dim)
    return block


def spectral_filter(rows_data, loc_spectrum):
    length_x = rows_data.shape[1]
    kept_waves = loc_spectrum.shape[0]
    freq_block = math.gcd(kept_waves, 256)
    positions = jnp.arange(length_x, dtype=jnp.int32)
    filtered = jnp.zeros(rows_data.shape, jnp.float32)
    for start_wave in range(0, kept_waves, freq_block):
        waves = start_wave + jnp.arange(freq_block, dtype=jnp.int32)
        phases = positions[:, None] * waves[None, :] % length_x
        radians = 2.0 * math.pi / length_x * phases.astype(jnp.float32)
        fourier_basis = jnp.concatenate([jnp.cos(radians), jnp.sin(radians)], axis=1)
        weights = loc_spectrum[start_wave : start_wave + freq_block]
        weights = jnp.concatenate([weights, weights])
        coeffs = jnp.dot(
            rows_data,
            fourier_basis,
            precision=lax.Precision.HIGHEST,
            preferred_element_type=jnp.float32,
        )
        filtered = filtered + jnp.dot(
            coeffs * weights[None, :],
            fourier_basis.T,
            precision=lax.Precision.HIGHEST,
            preferred_element_type=jnp.float32,
        )
    return filtered


def inner(field):
    return field[..., 1:-1, 1:-1]


def diff_x(field):
    return 0.5 * (field[..., 1:-1, 2:] - field[..., 1:-1, :-2])


def diff_y(field):
    return 0.5 * (field[..., 2:, 1:-1] - field[..., :-2, 1:-1])


def clip_rows(stack, margin, first_row, total_rows):
    rows_index = first_row - margin + jnp.arange(stack.shape[1], dtype=jnp.int32)
    valid = jnp.logical_and(rows_index >= 0, rows_index < total_rows).astype(jnp.float32)
    return stack * valid[None, :, None]


def coriolis_rows(first_row, margin, count, total_rows):
    rows_index = first_row - margin + jnp.arange(count, dtype=jnp.int32)
    return (0.1 + 0.2 * (rows_index.astype(jnp.float32) + 0.5) / total_rows)[:, None]


def forward_a(stack, margin, first_row, total_rows):
    height, eastward, northward = (stack[0], stack[1], stack[2])
    new_height = inner(height) - courant * (diff_x(eastward) + diff_y(northward))
    result = jnp.stack([new_height, inner(eastward), inner(northward)])
    return clip_rows(result, margin - 1, first_row, total_rows)


def forward_b(stack, margin, first_row, total_rows):
    height, eastward, northward = (stack[0], stack[1], stack[2])
    rotation = coriolis_rows(first_row, margin - 1, stack.shape[1] - 2, total_rows)
    new_east = inner(eastward) - courant * diff_x(height) + rotation * inner(northward)
    new_north = inner(northward) - courant * diff_y(height) - rotation * inner(eastward)
    result = jnp.stack([inner(height), new_east, new_north])
    return clip_rows(result, margin - 1, first_row, total_rows)


def backward_a(stack, margin, first_row, total_rows):
    back_h, back_u, back_w = (stack[0], stack[1], stack[2])
    adj_height = inner(back_h) + courant * (diff_x(back_u) + diff_y(back_w))
    result = jnp.stack([adj_height, inner(back_u), inner(back_w)])
    return clip_rows(result, margin - 1, first_row, total_rows)


def backward_b(stack, margin, first_row, total_rows):
    adj_height, back_u, back_w = (stack[0], stack[1], stack[2])
    rotation = coriolis_rows(first_row, margin - 1, stack.shape[1] - 2, total_rows)
    adj_east = inner(back_u) - rotation * inner(back_w) + courant * diff_x(adj_height)
    adj_north = inner(back_w) + rotation * inner(back_u) + courant * diff_y(adj_height)
    result = jnp.stack([inner(adj_height), adj_east, adj_north])
    return clip_rows(result, margin - 1, first_row, total_rows)


def deep_rim(stack):
    return extended(stack, (("grp", 1), ("sp", 2)), 4)


def per_device(
    alpha, ensemble, static_std, control, loc_spectrum, obs_cell, obs_step, innovation, obs_weight
):
    members_local = alpha.shape[0]
    groups = lax.axis_size("grp")
    spread = 1.0 / math.sqrt(members_local * groups - 1)
    tile_rows, tile_cols = (control.shape[1], control.shape[2])
    total_rows = tile_rows * groups
    first_row = lax.axis_index("grp") * tile_rows
    first_col = lax.axis_index("sp") * tile_cols

    def localize_items(items):
        dims = items.shape
        flat = items.reshape(dims[0] * dims[1], dims[2])
        return spectral_filter(flat, loc_spectrum).reshape(dims)

    def to_rows(columns):
        return localize_items(
            lax.all_to_all(columns, "sp", split_axis=1, concat_axis=2, tiled=True)
        )

    localized = lax.all_to_all(
        to_rows(alpha).astype(jnp.bfloat16), "sp", split_axis=2, concat_axis=1, tiled=True
    )
    partial_value = jnp.einsum(
        "mvyx,myx->vyx", ensemble, localized, preferred_element_type=jnp.float32
    )
    summed = lax.psum_scatter(partial_value, "grp", scatter_dimension=1, tiled=True)
    increment = static_std * control + spread * summed
    padded = clip_rows(deep_rim(increment), 4, first_row, total_rows)
    middle = forward_b(forward_a(padded, 4, first_row, total_rows), 3, first_row, total_rows)
    first_state = middle[:, 2:-2, 2:-2]
    second_state = forward_b(forward_a(middle, 2, first_row, total_rows), 1, first_row, total_rows)
    states = (increment, first_state, second_state)
    local_index = (obs_cell // NX - first_row) * tile_cols + (obs_cell % NX - first_col)
    observed = jnp.zeros(innovation.shape, jnp.float32)
    for moment in range(3):
        values = states[moment][0].reshape(-1)[local_index]
        observed = jnp.where(obs_step == moment, values, observed)
    misfit = obs_weight * (observed - innovation)
    forcings = []
    for moment in range(3):
        spread_obs = jnp.where(obs_step == moment, misfit, jnp.zeros_like(misfit))
        height_force = (
            jnp.zeros((tile_rows * tile_cols,), jnp.float32).at[local_index].add(spread_obs)
        )
        forcings.append(height_force.reshape(tile_rows, tile_cols))
    zero_field = jnp.zeros((tile_rows, tile_cols), jnp.float32)
    last_adjoint = jnp.stack([forcings[2], zero_field, zero_field])
    padded = clip_rows(
        deep_rim(jnp.concatenate([last_adjoint, forcings[1][None]], axis=0)),
        4,
        first_row,
        total_rows,
    )
    middle = backward_b(backward_a(padded[:3], 4, first_row, total_rows), 3, first_row, total_rows)
    middle = middle.at[0].add(padded[3, 2:-2, 2:-2])
    adjoint = backward_b(backward_a(middle, 2, first_row, total_rows), 1, first_row, total_rows)
    adjoint = adjoint.at[0].add(forcings[0])
    grad_control = control + static_std * adjoint
    half = adjoint.astype(jnp.bfloat16)
    weighted = jnp.einsum(
        "mvyx,vyx->myx",
        ensemble,
        lax.all_gather(half, "grp", axis=1, tiled=True),
        preferred_element_type=jnp.float32,
    )
    filtered = lax.all_to_all(to_rows(weighted), "sp", split_axis=2, concat_axis=1, tiled=True)
    grad_alpha = alpha + spread * filtered
    return (grad_alpha, grad_control)


def solution(mesh):
    placed = (
        P("grp", None, "sp"),
        P("grp", None, None, "sp"),
        P(None, "grp", "sp"),
        P(None, "grp", "sp"),
        P(),
        P(("grp", "sp")),
        P(("grp", "sp")),
        P(("grp", "sp")),
        P(("grp", "sp")),
    )
    return jax.shard_map(
        per_device,
        mesh=mesh,
        in_specs=placed,
        out_specs=(P("grp", None, "sp"), P(None, "grp", "sp")),
        check_vma=False,
    )
```

profile of v0, /device:TPU:0, one launch (start us, length us, event | category | flops | bytes accessed | tf_op | source)
XLA Modules:
  0.0 365.8 jit_solution(6767588958854362796)
XLA Ops:
  8.9 7.4 %all-to-all-start = ((f32[10,16,256]{2,0,1:T(8,128)}), f32[10,16,256]{2,0,1:T(8,128)S(1)}, u32[]{:S(2)}, u32[]{:S(2)}) async-start(f32[10,16,256]{2,0,1:T(8,128)} %copy.22), calls=%async_computation | async-start | bytes 524288 | tf_op jit(solution)/shard_map/all_to_all | solution.py:130
  16.3 17.6 %fusion.37 = (f32[4096,256]{1,0:T(8,128)}, f32[4096,256]{1,0:T(8,128)}) fusion(), kind=kLoop, calls=%fused_computation.65 | loop fusion | flops 14680064 | bytes 8388608 | tf_op jit(solution)/shard_map/sin | solution.py:35
  34.0 17.9 %fusion.44 = (f32[4096,256]{1,0:T(8,128)}, f32[4096,256]{1,0:T(8,128)}) fusion(s32[256]{0:T(256)S(1)} %iota_add_fusion.2), kind=kLoop, calls=%fused_computation.72 | loop fusion | flops 14680064 | bytes 8389632 | tf_op jit(solution)/shard_map/cos | solution.py:35
  51.8 17.9 %fusion.42 = (f32[4096,256]{1,0:T(8,128)}, f32[4096,256]{1,0:T(8,128)}) fusion(s32[256]{0:T(256)S(1)} %iota_add_fusion.1), kind=kLoop, calls=%fused_computation.70 | loop fusion | flops 14680064 | bytes 8389632 | tf_op jit(solution)/shard_map/cos | solution.py:35
  69.7 17.9 %fusion.40 = (f32[4096,256]{1,0:T(8,128)}, f32[4096,256]{1,0:T(8,128)}) fusion(s32[256]{0:T(256)S(1)} %iota_add_fusion), kind=kLoop, calls=%fused_computation.68 | loop fusion | flops 14680064 | bytes 8389632 | tf_op jit(solution)/shard_map/cos | solution.py:35
  88.0 7.5 %fusion.45 = f32[512,10]{0,1:T(8,128)S(1)} fusion(f32[10,4096]{1,0:T(8,128)S(1)} %bitcast.175, f32[4096,256]{1,0:T(8,128)} %get-tuple-element.106, f32[4096,256]{1,0:T(8,128)} %get-tuple-element.107, f32[512]{0:T(512)S(1)} %get-tuple-element.102), kind=kOutput, calls=%fused_computation.73 | convolution fusion | flops 253760512 | bytes 8574976 | tf_op jit(solution)/shard_map/dot_general | solution.py:38
  95.5 7.0 %fusion.35 = f32[10,4096]{1,0:T(8,128)S(1)} fusion(f32[512,10]{0,1:T(8,128)S(1)} %fusion.45, f32[4096,256]{1,0:T(8,128)S(1)} %copy-done, f32[4096,256]{1,0:T(8,128)S(1)} %copy-done.2), kind=kOutput, calls=%fused_computation.63 | convolution fusion | flops 253755392 | bytes 8572928 | tf_op jit(solution)/shard_map/dot_general | solution.py:44
  102.5 4.5 %fusion.47 = f32[512,10]{0,1:T(8,128)S(1)} fusion(f32[10,4096]{1,0:T(8,128)S(1)} %bitcast.176, f32[4096,256]{1,0:T(8,128)S(1)} %copy-done.14, f32[4096,256]{1,0:T(8,128)S(1)} %copy-done.12, f32[512]{0:T(512)S(1)} %get-tuple-element.103), kind=kOutput, calls=%fused_computation.75 | convolution fusion | flops 253760512 | bytes 8574976 | tf_op jit(solution)/shard_map/dot_general | solution.py:38
  107.0 7.2 %convolution_add_fusion.5 = f32[10,4096]{1,0:T(8,128)S(1)} fusion(f32[10,4096]{1,0:T(8,128)S(1)} %fusion.35, f32[512,10]{0,1:T(8,128)S(1)} %fusion.47, f32[4096,256]{1,0:T(8,128)S(1)} %copy-done.14, f32[4096,256]{1,0:T(8,128)S(1)} %copy-done.12), kind=kOutput, calls=%fused_computation.28 | convolution fusion | flops 253796352 | bytes 8736768 | tf_op jit(solution)/shard_map/dot_general | solution.py:44
  114.2 4.5 %fusion.49 = f32[512,10]{0,1:T(8,128)S(1)} fusion(f32[10,4096]{1,0:T(8,128)S(1)} %bitcast.177, f32[4096,256]{1,0:T(8,128)S(1)} %copy-done.10, f32[4096,256]{1,0:T(8,128)S(1)} %copy-done.8, f32[512]{0:T(512)S(1)} %get-tuple-element.104), kind=kOutput, calls=%fused_computation.77 | convolution fusion | flops 253760512 | bytes 8574976 | tf_op jit(solution)/shard_map/dot_general | solution.py:38
  118.7 7.4 %convolution_add_fusion.4 = f32[10,4096]{1,0:T(8,128)S(1)} fusion(f32[10,4096]{1,0:T(8,128)S(1)} %convolution_add_fusion.5, f32[512,10]{0,1:T(8,128)S(1)} %fusion.49, f32[4096,256]{1,0:T(8,128)S(1)} %copy-done.10, f32[4096,256]{1,0:T(8,128)S(1)} %copy-done.8), kind=kOutput, calls=%fused_computation.27 | convolution fusion | flops 253796352 | bytes 8736768 | tf_op jit(solution)/shard_map/dot_general | solution.py:44
  126.2 4.5 %fusion.51 = f32[512,10]{0,1:T(8,128)S(1)} fusion(f32[10,4096]{1,0:T(8,128)S(1)} %bitcast.178, f32[4096,256]{1,0:T(8,128)S(1)} %copy-done.6, f32[4096,256]{1,0:T(8,128)S(1)} %copy-done.4, f32[512]{0:T(512)S(1)} %get-tuple-element.105), kind=kOutput, calls=%fused_computation.79 | convolution fusion | flops 253760512 | bytes 8574976 | tf_op jit(solution)/shard_map/dot_general | solution.py:38
  130.7 7.2 %fusion.2 = bf16[10,1,4096]{2,0,1:T(8,128)(2,1)S(1)} fusion(f32[10,4096]{1,0:T(8,128)S(1)} %convolution_add_fusion.4, f32[512,10]{0,1:T(8,128)S(1)} %fusion.51, f32[4096,256]{1,0:T(8,128)S(1)} %copy-done.6, f32[4096,256]{1,0:T(8,128)S(1)} %copy-done.4), kind=kOutput, calls=%fused_computation.30 | convolution fusion | flops 253837312 | bytes 8654848 | tf_op jit(solution)/shard_map/dot_general | solution.py:44
  137.8 2.8 copy.24
  141.2 22.5 %reduce.10 = bf16[4096,10]{1,0:T(8,128)(2,1)S(1)} reduce(bf16[4096,1,10]{2,1,0:T(2,128)(2,1)S(1)} %bitcast.160, bf16[]{:T(256)} %broadcast.393), dimensions={1}, to_apply=%bitcast.136.reduce_sub_computation | reduce | bytes 163842
  163.6 2.5 reshape.233
  166.1 6.0 %all-to-all-start.1 = ((bf16[16,2,1280]{2,1,0:T(2,128)(2,1)}), bf16[16,2,1280]{2,1,0:T(2,128)(2,1)S(1)}, u32[]{:S(2)}, u32[]{:S(2)}) async-start(bf16[16,2,1280]{2,1,0:T(2,128)(2,1)} %reshape.233), calls=%async_computation.1 | async-start | bytes 163840 | tf_op jit(solution)/shard_map/all_to_all | solution.py:133
  172.2 7.0 %all-to-all-done.1 = bf16[16,2,1280]{2,1,0:T(2,128)(2,1)S(1)} async-done(((bf16[16,2,1280]{2,1,0:T(2,128)(2,1)}), bf16[16,2,1280]{2,1,0:T(2,128)(2,1)S(1)}, u32[]{:S(2)}, u32[]{:S(2)}) %all-to-all-start.1) | async-done | bytes 81952 | tf_op jit(solution)/shard_map/all_to_all | solution.py:133
  179.2 2.2 reshape.234
  181.4 2.1 copy.25
  184.4 7.6 %reduce-scatter.2.cloned.1.call-done = f32[3,8,256]{2,1,0:T(8,128)} async-done(((f32[3,16,256]{2,1,0:T(8,128)}), f32[3,8,256]{2,1,0:T(8,128)}) %reduce-scatter.2.cloned.1.call-update) | async-done | bytes 24592 | tf_op jit(solution)/shard_map/reduce_scatter | solution.py:139
  193.0 1.8 collective-permute-start.1
  196.8 4.4 %collective-permute-start.3 = (f32[3,16,4]{2,1,0:T(8,128)S(1)}, f32[3,16,4]{2,1,0:T(8,128)S(1)}, u32[]{:S(2)}, u32[]{:S(2)}) collective-permute-start(f32[3,16,4]{2,1,0:T(8,128)S(1)} %get-tuple-element.67), channel_id=1, source_target_pairs={{1,0},{2,1},{3,2},{4,3},{5,4},{6,5},{7,6},{8,7},{9,8},{10,9},{11,1... | collective-permute-start | bytes 2312 | tf_op jit(solution)/shard_map/ppermute | solution.py:20
  201.2 6.1 %gather_fusion.2 = f32[1024]{0:T(1024)S(1)} fusion(f32[2048]{0:T(1024)S(1)} %bitcast.158, s32[1024]{0:T(1024)S(1)} %get-tuple-element.30), kind=kCustom, calls=%fused_computation.2 | custom fusion | bytes 12288 | tf_op jit(solution)/shard_map/gather | solution.py:149
  208.4 6.2 %gather_fusion = f32[1024]{0:T(1024)S(1)} fusion(f32[2048]{0:T(1024)S(1)} %bitcast.159, s32[1024]{0:T(1024)S(1)} %get-tuple-element.30), kind=kCustom, calls=%fused_computation | custom fusion | bytes 12288 | tf_op jit(solution)/shard_map/gather | solution.py:149
  214.6 6.2 %gather_fusion.1 = f32[1024]{0:T(1024)S(1)} fusion(f32[2048]{0:T(1024)S(1)} %bitcast.157, s32[1024]{0:T(1024)S(1)} %get-tuple-element.30), kind=kCustom, calls=%fused_computation.1 | custom fusion | bytes 12288 | tf_op jit(solution)/shard_map/gather | solution.py:149
  220.8 6.0 %scatter_custom_fusion = f32[2048]{0:T(1024)S(1)} fusion(s32[1024]{0:T(1024)S(1)} %get-tuple-element.31, f32[1024]{0:T(1024)S(1)} %get-tuple-element.90, f32[]{:T(128)} %constant.175.clone.1), kind=kCustom, calls=%fused_computation.226 | custom fusion | flops 1024 | bytes 8196 | tf_op jit(solution)/shard_map/scatter-add | solution.py:156
  226.8 6.0 %scatter_custom_fusion.1 = f32[2048]{0:T(1024)S(1)} fusion(s32[1024]{0:T(1024)S(1)} %get-tuple-element.31, f32[1024]{0:T(1024)S(1)} %get-tuple-element.91, f32[]{:T(128)} %constant.175.clone.1), kind=kCustom, calls=%fused_computation.224 | custom fusion | flops 1024 | bytes 8196 | tf_op jit(solution)/shard_map/scatter-add | solution.py:156
  232.8 2.0 collective-permute-start.4
  236.6 1.9 collective-permute-done.5
  238.6 4.4 %collective-permute-start.7 = (f32[4,16,4]{2,1,0:T(8,128)S(1)}, f32[4,16,4]{2,1,0:T(8,128)S(1)}, u32[]{:S(2)}, u32[]{:S(2)}) collective-permute-start(f32[4,16,4]{2,1,0:T(8,128)S(1)} %get-tuple-element.65), channel_id=1, source_target_pairs={{1,0},{2,1},{3,2},{4,3},{5,4},{6,5},{7,6},{8,7},{9,8},{10,9},{11,1... | collective-permute-start | bytes 3080 | tf_op jit(solution)/shard_map/ppermute | solution.py:20
  243.0 6.0 %scatter_custom_fusion.2 = f32[2048]{0:T(1024)S(1)} fusion(s32[1024]{0:T(1024)S(1)} %get-tuple-element.31, f32[1024]{0:T(1024)S(1)} %get-tuple-element.26, f32[]{:T(128)} %constant.175.clone.1), kind=kCustom, calls=%fused_computation.222 | custom fusion | flops 1024 | bytes 8196 | tf_op jit(solution)/shard_map/scatter-add | solution.py:156
  250.6 4.4 %all_gather.3 = bf16[3,16,256]{2,1,0:T(8,128)(2,1)S(1)} all-gather(bf16[3,8,256]{2,1,0:T(8,128)(2,1)S(1)} %get-tuple-element.71), channel_id=1, replica_groups=mesh['grp'=2,'sp'=16] {'grp'}, dimensions={1}, use_global_device_ids=true | all-gather | bytes 36864 | tf_op jit(solution)/shard_map/all_gather | solution.py:176
  255.2 12.6 %all_to_all.19 = f32[10,16,256]{2,0,1:T(8,128)S(1)} all-to-all(f32[10,16,256]{2,0,1:T(8,128)S(1)} %bitcast.170), channel_id=1, replica_groups=mesh['grp'=2,'sp'=16] {'sp'}, dimensions={1} | all-to-all | bytes 327680 | tf_op jit(solution)/shard_map/all_to_all | solution.py:130
  268.1 4.9 %fusion.52 = f32[10,512]{1,0:T(8,128)S(1)} fusion(f32[10,4096]{1,0:T(8,128)S(1)} %bitcast.164, f32[4096,256]{1,0:T(8,128)} %get-tuple-element.97, f32[4096,256]{1,0:T(8,128)S(1)} %copy-done.5, f32[512]{0:T(512)S(1)} %get-tuple-element.105), kind=kOutput, calls=%fused_computation.80 | convolution fusion | flops 253760512 | bytes 8574976 | tf_op jit(solution)/shard_map/dot_general | solution.py:38
  273.1 4.1 %fusion.50 = f32[10,512]{1,0:T(8,128)S(1)} fusion(f32[10,4096]{1,0:T(8,128)S(1)} %bitcast.165, f32[4096,256]{1,0:T(8,128)S(1)} %copy-done.11, f32[4096,256]{1,0:T(8,128)S(1)} %copy-done.9, f32[512]{0:T(512)S(1)} %get-tuple-element.104), kind=kOutput, calls=%fused_computation.78 | convolution fusion | flops 253760512 | bytes 8574976 | tf_op jit(solution)/shard_map/dot_general | solution.py:38
  277.2 4.1 %fusion.48 = f32[10,512]{1,0:T(8,128)S(1)} fusion(f32[10,4096]{1,0:T(8,128)S(1)} %bitcast.166, f32[4096,256]{1,0:T(8,128)S(1)} %copy-done.15, f32[4096,256]{1,0:T(8,128)S(1)} %copy-done.13, f32[512]{0:T(512)S(1)} %get-tuple-element.103), kind=kOutput, calls=%fused_computation.76 | convolution fusion | flops 253760512 | bytes 8574976 | tf_op jit(solution)/shard_map/dot_general | solution.py:38
  281.3 4.3 %fusion.46 = f32[10,512]{1,0:T(8,128)S(1)} fusion(f32[10,4096]{1,0:T(8,128)S(1)} %bitcast.167, f32[4096,256]{1,0:T(8,128)S(1)} %copy-done.1, f32[4096,256]{1,0:T(8,128)S(1)} %copy-done.3, f32[512]{0:T(512)S(1)} %get-tuple-element.102), kind=kOutput, calls=%fused_computation.74 | convolution fusion | flops 253760512 | bytes 8574976 | tf_op jit(solution)/shard_map/dot_general | solution.py:38
  285.5 7.0 %fusion.33 = f32[10,4096]{1,0:T(8,128)S(1)} fusion(f32[10,512]{1,0:T(8,128)S(1)} %fusion.46, f32[4096,256]{1,0:T(8,128)S(1)} %copy-done.1, f32[4096,256]{1,0:T(8,128)S(1)} %copy-done.3), kind=kOutput, calls=%fused_computation.61 | convolution fusion | flops 253755392 | bytes 8572928 | tf_op jit(solution)/shard_map/dot_general | solution.py:44
  292.5 7.2 %convolution_add_fusion.2 = f32[10,4096]{1,0:T(8,128)S(1)} fusion(f32[10,4096]{1,0:T(8,128)S(1)} %fusion.33, f32[10,512]{1,0:T(8,128)S(1)} %fusion.48, f32[4096,256]{1,0:T(8,128)S(1)} %copy-done.15, f32[4096,256]{1,0:T(8,128)S(1)} %copy-done.13), kind=kOutput, calls=%fused_computation.25 | convolution fusion | flops 253796352 | bytes 8736768 | tf_op jit(solution)/shard_map/dot_general | solution.py:44
  299.7 7.0 %convolution_add_fusion.1 = f32[10,4096]{1,0:T(8,128)S(1)} fusion(f32[10,4096]{1,0:T(8,128)S(1)} %convolution_add_fusion.2, f32[10,512]{1,0:T(8,128)S(1)} %fusion.50, f32[4096,256]{1,0:T(8,128)S(1)} %copy-done.11, f32[4096,256]{1,0:T(8,128)S(1)} %copy-done.9), kind=kOutput, calls=%fused_computation.24 | convolution fusion | flops 253796352 | bytes 8736768 | tf_op jit(solution)/shard_map/dot_general | solution.py:44
  306.7 7.0 %fusion = f32[10,1,4096]{2,0,1:T(8,128)S(1)} fusion(f32[10,4096]{1,0:T(8,128)S(1)} %convolution_add_fusion.1, f32[10,512]{1,0:T(8,128)S(1)} %fusion.52, f32[4096,256]{1,0:T(8,128)S(1)} %copy-done.7, f32[4096,256]{1,0:T(8,128)S(1)} %copy-done.5), kind=kOutput, calls=%fused_computation.23 | convolution fusion | flops 253796352 | bytes 8736768 | tf_op jit(solution)/shard_map/dot_general | solution.py:44
  313.7 2.5 copy.27
  316.7 19.6 %reduce.11 = f32[4096,10]{1,0:T(8,128)} reduce(f32[4096,1,10]{2,1,0:T(1,128)S(1)} %bitcast.161, f32[]{:T(128)} %broadcast.394), dimensions={1}, to_apply=%bitcast.138.reduce_sub_computation | reduce | bytes 327684
  336.4 3.4 reshape.235
  339.8 11.1 %all_to_all.40 = f32[16,1,2560]{2,1,0:T(1,128)S(1)} all-to-all(f32[16,1,2560]{2,1,0:T(1,128)S(1)} %reshape.235), channel_id=1, replica_groups=mesh['grp'=2,'sp'=16] {'sp'}, dimensions={0} | all-to-all | bytes 327680 | tf_op jit(solution)/shard_map/all_to_all | solution.py:179
  352.0 3.3 reshape.236
  355.2 2.0 copy.28
  (144 shorter events, 14.2 us)
Async XLA Ops:
  8.9 78.7 %all-to-all-start = ((f32[10,16,256]{2,0,1:T(8,128)}), f32[10,16,256]{2,0,1:T(8,128)S(1)}, u32[]{:S(2)}, u32[]{:S(2)}) async-start(f32[10,16,256]{2,0,1:T(8,128)} %copy.22), calls=%async_computation | async-start | bytes 524288 | tf_op jit(solution)/shard_map/all_to_all | solution.py:130
  16.3 17.7 %copy-start.23 = (f32[1024]{0:T(1024)S(1)}, f32[1024]{0:T(1024)}, u32[]{:S(2)}) copy-start(f32[1024]{0:T(1024)} %param.17) | copy-start | bytes 12292
  69.7 17.9 %copy-start.24 = (s32[1024]{0:T(1024)S(1)}, s32[1024]{0:T(1024)}, u32[]{:S(2)}) copy-start(s32[1024]{0:T(1024)} %param.18) | copy-start | bytes 12292
  87.9 7.5 %copy-start = (f32[4096,256]{1,0:T(8,128)S(1)}, f32[4096,256]{1,0:T(8,128)}, u32[]{:S(2)}) copy-start(f32[4096,256]{1,0:T(8,128)} %get-tuple-element.106) | copy-start | bytes 12582916
  87.9 7.5 %copy-start.2 = (f32[4096,256]{1,0:T(8,128)S(1)}, f32[4096,256]{1,0:T(8,128)}, u32[]{:S(2)}) copy-start(f32[4096,256]{1,0:T(8,128)} %get-tuple-element.107) | copy-start | bytes 12582916
  95.5 7.0 %copy-start.12 = (f32[4096,256]{1,0:T(8,128)S(1)}, f32[4096,256]{1,0:T(8,128)}, u32[]{:S(2)}) copy-start(f32[4096,256]{1,0:T(8,128)} %get-tuple-element.100) | copy-start | bytes 12582916
  95.5 7.0 %copy-start.14 = (f32[4096,256]{1,0:T(8,128)S(1)}, f32[4096,256]{1,0:T(8,128)}, u32[]{:S(2)}) copy-start(f32[4096,256]{1,0:T(8,128)} %get-tuple-element.101) | copy-start | bytes 12582916
  107.0 7.2 %copy-start.8 = (f32[4096,256]{1,0:T(8,128)S(1)}, f32[4096,256]{1,0:T(8,128)}, u32[]{:S(2)}) copy-start(f32[4096,256]{1,0:T(8,128)} %get-tuple-element.98) | copy-start | bytes 12582916
  107.0 7.2 %copy-start.10 = (f32[4096,256]{1,0:T(8,128)S(1)}, f32[4096,256]{1,0:T(8,128)}, u32[]{:S(2)}) copy-start(f32[4096,256]{1,0:T(8,128)} %get-tuple-element.99) | copy-start | bytes 12582916
  118.7 7.4 %copy-start.4 = (f32[4096,256]{1,0:T(8,128)S(1)}, f32[4096,256]{1,0:T(8,128)}, u32[]{:S(2)}) copy-start(f32[4096,256]{1,0:T(8,128)} %get-tuple-element.96) | copy-start | bytes 12582916
  118.7 7.4 %copy-start.6 = (f32[4096,256]{1,0:T(8,128)S(1)}, f32[4096,256]{1,0:T(8,128)}, u32[]{:S(2)}) copy-start(f32[4096,256]{1,0:T(8,128)} %get-tuple-element.97) | copy-start | bytes 12582916
  141.2 42.5 %copy-start.16 = (bf16[10,3,16,256]{3,2,1,0:T(8,128)(2,1)S(1)}, bf16[10,3,16,256]{3,2,1,0:T(8,128)(2,1)}, u32[]{:S(2)}) copy-start(bf16[10,3,16,256]{3,2,1,0:T(8,128)(2,1)} %param.14) | copy-start | bytes 737284
  141.2 50.8 %copy-start.18 = (f32[3,8,256]{2,1,0:T(8,128)S(1)}, f32[3,8,256]{2,1,0:T(8,128)}, u32[]{:S(2)}) copy-start(f32[3,8,256]{2,1,0:T(8,128)} %param.16) | copy-start | bytes 73732
  141.2 50.8 %copy-start.19 = (f32[3,8,256]{2,1,0:T(8,128)S(1)}, f32[3,8,256]{2,1,0:T(8,128)}, u32[]{:S(2)}) copy-start(f32[3,8,256]{2,1,0:T(8,128)} %param.15) | copy-start | bytes 73732
  166.1 13.1 %all-to-all-start.1 = ((bf16[16,2,1280]{2,1,0:T(2,128)(2,1)}), bf16[16,2,1280]{2,1,0:T(2,128)(2,1)S(1)}, u32[]{:S(2)}, u32[]{:S(2)}) async-start(bf16[16,2,1280]{2,1,0:T(2,128)(2,1)} %reshape.233), calls=%async_computation.1 | async-start | bytes 163840 | tf_op jit(solution)/shard_map/all_to_all | solution.py:133
  172.1 19.9 %reduce-scatter.2.cloned.1.call-start = ((), (), s32[]{:S(2)}) async-start(), calls=%async_computation.5 | async-start | bytes 73728 | tf_op jit(solution)/shard_map/reduce_scatter | solution.py:139
  192.7 3.8 %collective-permute-start = (f32[3,4,256]{2,1,0:T(4,128)S(1)}, f32[3,4,256]{2,1,0:T(4,128)S(1)}, u32[]{:S(2)}, u32[]{:S(2)}) collective-permute-start(f32[3,4,256]{2,1,0:T(4,128)S(1)} %get-tuple-element.88), channel_id=1, source_target_pairs={{0,16},{16,0},{1,17},{17,1},{2,18},{18,2},{3,19},{19,3},{4,20},{20... | collective-permute-start | bytes 36872 | tf_op jit(solution)/shard_map/ppermute | solution.py:17
  193.0 3.7 %collective-permute-start.1 = (f32[3,4,256]{2,1,0:T(4,128)S(1)}, f32[3,4,256]{2,1,0:T(4,128)S(1)}, u32[]{:S(2)}, u32[]{:S(2)}) collective-permute-start(f32[3,4,256]{2,1,0:T(4,128)S(1)} %get-tuple-element.89), channel_id=1, source_target_pairs={{16,0},{0,16},{17,1},{1,17},{18,2},{2,18},{19,3},{3,19},{20,4},{4,... | collective-permute-start | bytes 36872 | tf_op jit(solution)/shard_map/ppermute | solution.py:20
  196.7 10.6 %collective-permute-start.2 = (f32[3,16,4]{2,1,0:T(8,128)S(1)}, f32[3,16,4]{2,1,0:T(8,128)S(1)}, u32[]{:S(2)}, u32[]{:S(2)}) collective-permute-start(f32[3,16,4]{2,1,0:T(8,128)S(1)} %get-tuple-element.66), channel_id=1, source_target_pairs={{0,1},{1,2},{2,3},{3,4},{4,5},{5,6},{6,7},{7,8},{8,9},{9,10},{10,1... | collective-permute-start | bytes 2312 | tf_op jit(solution)/shard_map/ppermute | solution.py:17
  196.8 10.6 %collective-permute-start.3 = (f32[3,16,4]{2,1,0:T(8,128)S(1)}, f32[3,16,4]{2,1,0:T(8,128)S(1)}, u32[]{:S(2)}, u32[]{:S(2)}) collective-permute-start(f32[3,16,4]{2,1,0:T(8,128)S(1)} %get-tuple-element.67), channel_id=1, source_target_pairs={{1,0},{2,1},{3,2},{4,3},{5,4},{6,5},{7,6},{8,7},{9,8},{10,9},{11,1... | collective-permute-start | bytes 2312 | tf_op jit(solution)/shard_map/ppermute | solution.py:20
  208.4 12.4 %copy-start.20 = (f32[1024]{0:T(1024)S(1)}, f32[1024]{0:T(1024)}, u32[]{:S(2)}) copy-start(f32[1024]{0:T(1024)} %param.21) | copy-start | bytes 12292
  208.4 12.4 %copy-start.21 = (f32[1024]{0:T(1024)S(1)}, f32[1024]{0:T(1024)}, u32[]{:S(2)}) copy-start(f32[1024]{0:T(1024)} %param.20) | copy-start | bytes 12292
  208.4 12.4 %copy-start.22 = (s32[1024]{0:T(1024)S(1)}, s32[1024]{0:T(1024)}, u32[]{:S(2)}) copy-start(s32[1024]{0:T(1024)} %param.19) | copy-start | bytes 12292
  232.8 3.8 %collective-permute-start.4 = (f32[4,4,256]{2,1,0:T(4,128)S(1)}, f32[4,4,256]{2,1,0:T(4,128)S(1)}, u32[]{:S(2)}, u32[]{:S(2)}) collective-permute-start(f32[4,4,256]{2,1,0:T(4,128)S(1)} %get-tuple-element.68), channel_id=1, source_target_pairs={{0,16},{16,0},{1,17},{17,1},{2,18},{18,2},{3,19},{19,3},{4,20},{20... | collective-permute-start | bytes 49160 | tf_op jit(solution)/shard_map/ppermute | solution.py:17
  234.7 3.7 %collective-permute-start.5 = (f32[4,4,256]{2,1,0:T(4,128)S(1)}, f32[4,4,256]{2,1,0:T(4,128)S(1)}, u32[]{:S(2)}, u32[]{:S(2)}) collective-permute-start(f32[4,4,256]{2,1,0:T(4,128)S(1)} %get-tuple-element.69), channel_id=1, source_target_pairs={{16,0},{0,16},{17,1},{1,17},{18,2},{2,18},{19,3},{3,19},{20,4},{4,... | collective-permute-start | bytes 49160 | tf_op jit(solution)/shard_map/ppermute | solution.py:20
  238.6 10.4 %collective-permute-start.6 = (f32[4,16,4]{2,1,0:T(8,128)S(1)}, f32[4,16,4]{2,1,0:T(8,128)S(1)}, u32[]{:S(2)}, u32[]{:S(2)}) collective-permute-start(f32[4,16,4]{2,1,0:T(8,128)S(1)} %get-tuple-element.64), channel_id=1, source_target_pairs={{0,1},{1,2},{2,3},{3,4},{4,5},{5,6},{6,7},{7,8},{8,9},{9,10},{10,1... | collective-permute-start | bytes 3080 | tf_op jit(solution)/shard_map/ppermute | solution.py:17
  238.6 10.4 %collective-permute-start.7 = (f32[4,16,4]{2,1,0:T(8,128)S(1)}, f32[4,16,4]{2,1,0:T(8,128)S(1)}, u32[]{:S(2)}, u32[]{:S(2)}) collective-permute-start(f32[4,16,4]{2,1,0:T(8,128)S(1)} %get-tuple-element.65), channel_id=1, source_target_pairs={{1,0},{2,1},{3,2},{4,3},{5,4},{6,5},{7,6},{8,7},{9,8},{10,9},{11,1... | collective-permute-start | bytes 3080 | tf_op jit(solution)/shard_map/ppermute | solution.py:20
  249.0 19.1 %copy-start.5 = (f32[4096,256]{1,0:T(8,128)S(1)}, f32[4096,256]{1,0:T(8,128)}, u32[]{:S(2)}) copy-start(f32[4096,256]{1,0:T(8,128)} %get-tuple-element.96) | copy-start | bytes 12582916
  268.1 4.9 %copy-start.9 = (f32[4096,256]{1,0:T(8,128)S(1)}, f32[4096,256]{1,0:T(8,128)}, u32[]{:S(2)}) copy-start(f32[4096,256]{1,0:T(8,128)} %get-tuple-element.98) | copy-start | bytes 12582916
  268.1 4.9 %copy-start.11 = (f32[4096,256]{1,0:T(8,128)S(1)}, f32[4096,256]{1,0:T(8,128)}, u32[]{:S(2)}) copy-start(f32[4096,256]{1,0:T(8,128)} %get-tuple-element.99) | copy-start | bytes 12582916
  273.0 4.1 %copy-start.13 = (f32[4096,256]{1,0:T(8,128)S(1)}, f32[4096,256]{1,0:T(8,128)}, u32[]{:S(2)}) copy-start(f32[4096,256]{1,0:T(8,128)} %get-tuple-element.100) | copy-start | bytes 12582916
  273.1 4.1 %copy-start.15 = (f32[4096,256]{1,0:T(8,128)S(1)}, f32[4096,256]{1,0:T(8,128)}, u32[]{:S(2)}) copy-start(f32[4096,256]{1,0:T(8,128)} %get-tuple-element.101) | copy-start | bytes 12582916
  277.2 4.1 %copy-start.1 = (f32[4096,256]{1,0:T(8,128)S(1)}, f32[4096,256]{1,0:T(8,128)}, u32[]{:S(2)}) copy-start(f32[4096,256]{1,0:T(8,128)} %get-tuple-element.106) | copy-start | bytes 12582916
  277.2 4.1 %copy-start.3 = (f32[4096,256]{1,0:T(8,128)S(1)}, f32[4096,256]{1,0:T(8,128)}, u32[]{:S(2)}) copy-start(f32[4096,256]{1,0:T(8,128)} %get-tuple-element.107) | copy-start | bytes 12582916
  299.7 7.0 %copy-start.7 = (f32[4096,256]{1,0:T(8,128)S(1)}, f32[4096,256]{1,0:T(8,128)}, u32[]{:S(2)}) copy-start(f32[4096,256]{1,0:T(8,128)} %get-tuple-element.97) | copy-start | bytes 12582916
  336.4 21.4 %copy-start.17 = (f32[10,16,256]{2,1,0:T(8,128)S(1)}, f32[10,16,256]{2,1,0:T(8,128)}, u32[]{:S(2)}) copy-start(f32[10,16,256]{2,1,0:T(8,128)} %param.13) | copy-start | bytes 491524
Sparse Core Ops, SparseCore 0:
  184.5 7.4 reduce-scatter.1
where the time goes:
time: 372 us; the launch traced here: 366 us
  other arithmetic  137 us (37%)
  matrix products  95.2 us (26%)
  local copies, waits for them, and re-layouts  43.3 us (12%)
  blocking collectives  28.1 us (8%)
  starting transfers between devices  26.5 us (7%)
  waiting for transfers between devices  20.1 us (5%)
  between operations  15.3 us (4%)
    dot_general x8, matrix products, spectral_filter(): jnp.dot(coeffs * weights[None, :], fourier_basis.T, precision=lax.Precisi...  56.9 us
    cos x3, other arithmetic, spectral_filter(): jnp.cos(radians)  53.6 us
    unnamed x6, other arithmetic  42.2 us
    dot_general x8, matrix products, spectral_filter(): jnp.dot(rows_data, fourier_basis, precision=lax.Precision.HIGHEST, prefer...  38.3 us
    gather x3, local copies, waits for them, and re-layouts, per_device(): values = states[moment][0].reshape(-1)[local_index]  18.5 us
    scatter-add x3, other arithmetic, per_device(): jnp.zeros((tile_rows * tile_cols,), jnp.float32).at[local_index]  17.9 us
    sin x1, other arithmetic, spectral_filter(): jnp.sin(radians)  17.6 us
    unnamed x68, local copies, waits for them, and re-layouts  14.9 us
  transfers between devices with their start and end apart: 11, of which 6 were waited for; matrix products, arithmetic and copies ran while one was open for 23% of the time, Pallas kernels for 0%

commit v1 on v0

--- a/solution.py
+++ b/solution.py
@@ -3,6 +3,7 @@
 import jax.numpy as jnp
 from jax import lax
 from jax.sharding import PartitionSpec as P
+from jax.lax import all_to_all, axis_size
 
 NX = 4096
 courant = 0.4
@@ -176,7 +177,16 @@
         lax.all_gather(half, "grp", axis=1, tiled=True),
         preferred_element_type=jnp.float32,
     )
-    filtered = lax.all_to_all(to_rows(weighted), "sp", split_axis=2, concat_axis=1, tiled=True)
+    incoming_x = to_rows(weighted)
+    filtered = jnp.concatenate(
+        all_to_all(
+            jnp.stack(jnp.split(incoming_x, axis_size("sp"), axis=2)),
+            axis_name="sp",
+            split_axis=0,
+            concat_axis=0,
+        ),
+        axis=1,
+    )
     grad_alpha = alpha + spread * filtered
     return (grad_alpha, grad_control)
 

time: 372 us -> 339 us (0.911)
  other arithmetic: 137 us -> 116 us
  local copies, waits for them, and re-layouts: 43.3 us -> 31.8 us
    unnamed x6 -> x5, other arithmetic: 42.2 us -> 22.6 us
    unnamed x68 -> x79, local copies, waits for them, and re-layouts: 14.9 us -> 7.67 us
  transfers between devices with their start and end apart: 11 -> 11, of which waited for: 6 -> 6; matrix products, arithmetic and copies ran while one was open for 23% -> 25% of each run, Pallas kernels for 0% -> 0%
where the time goes in v1:
time: 339 us; the launch traced here: 333 us
  other arithmetic  116 us (34%)
  matrix products  95.2 us (28%)
  local copies, waits for them, and re-layouts  31.8 us (9%)
  blocking collectives  28.1 us (8%)
  starting transfers between devices  26.5 us (8%)
  waiting for transfers between devices  20.1 us (6%)
  between operations  15.2 us (4%)
    dot_general x8, matrix products, spectral_filter(): jnp.dot(coeffs * weights[None, :], fourier_basis.T, precision=lax.Precisi...  56.9 us
    cos x3, other arithmetic, spectral_filter(): jnp.cos(radians)  53.6 us
    dot_general x8, matrix products, spectral_filter(): jnp.dot(rows_data, fourier_basis, precision=lax.Precision.HIGHEST, prefer...  38.3 us
    unnamed x5, other arithmetic  22.6 us
    gather x3, local copies, waits for them, and re-layouts, per_device(): values = states[moment][0].reshape(-1)[local_index]  18.5 us
    scatter-add x3, other arithmetic, per_device(): jnp.zeros((tile_rows * tile_cols,), jnp.float32).at[local_index]  17.9 us
    sin x1, other arithmetic, spectral_filter(): jnp.sin(radians)  17.6 us
    all_to_all x1, blocking collectives, to_rows(): lax.all_to_all(columns, 'sp', split_axis=1, concat_axis=2, tiled=True)  12.6 us
  transfers between devices with their start and end apart: 11, of which 6 were waited for; matrix products, arithmetic and copies ran while one was open for 25% of the time, Pallas kernels for 0%

profile of v1, /device:TPU:0, one launch (start us, length us, event | category | flops | bytes accessed | tf_op | source)
XLA Modules:
  0.0 333.0 jit_solution(13416457618077398377)
XLA Ops:
  7.2 1.7 copy.20
  8.9 7.4 %all-to-all-start = ((f32[10,16,256]{2,0,1:T(8,128)}), f32[10,16,256]{2,0,1:T(8,128)S(1)}, u32[]{:S(2)}, u32[]{:S(2)}) async-start(f32[10,16,256]{2,0,1:T(8,128)} %copy.20), calls=%async_computation | async-start | bytes 524288 | tf_op jit(solution)/shard_map/all_to_all | solution.py:131
  16.3 17.6 %fusion.37 = (f32[4096,256]{1,0:T(8,128)}, f32[4096,256]{1,0:T(8,128)}) fusion(), kind=kLoop, calls=%fused_computation.65 | loop fusion | flops 14680064 | bytes 8388608 | tf_op jit(solution)/shard_map/sin | solution.py:36
  34.0 17.9 %fusion.44 = (f32[4096,256]{1,0:T(8,128)}, f32[4096,256]{1,0:T(8,128)}) fusion(s32[256]{0:T(256)S(1)} %iota_add_fusion.2), kind=kLoop, calls=%fused_computation.72 | loop fusion | flops 14680064 | bytes 8389632 | tf_op jit(solution)/shard_map/cos | solution.py:36
  51.8 17.9 %fusion.42 = (f32[4096,256]{1,0:T(8,128)}, f32[4096,256]{1,0:T(8,128)}) fusion(s32[256]{0:T(256)S(1)} %iota_add_fusion.1), kind=kLoop, calls=%fused_computation.70 | loop fusion | flops 14680064 | bytes 8389632 | tf_op jit(solution)/shard_map/cos | solution.py:36
  69.7 17.8 %fusion.40 = (f32[4096,256]{1,0:T(8,128)}, f32[4096,256]{1,0:T(8,128)}) fusion(s32[256]{0:T(256)S(1)} %iota_add_fusion), kind=kLoop, calls=%fused_computation.68 | loop fusion | flops 14680064 | bytes 8389632 | tf_op jit(solution)/shard_map/cos | solution.py:36
  88.0 7.5 %fusion.45 = f32[512,10]{0,1:T(8,128)S(1)} fusion(f32[10,4096]{1,0:T(8,128)S(1)} %bitcast.234, f32[4096,256]{1,0:T(8,128)} %get-tuple-element.112, f32[4096,256]{1,0:T(8,128)} %get-tuple-element.113, f32[512]{0:T(512)S(1)} %get-tuple-element.108), kind=kOutput, calls=%fused_computation.73 | convolution fusion | flops 253760512 | bytes 8574976 | tf_op jit(solution)/shard_map/dot_general | solution.py:39
  95.5 7.0 %fusion.35 = f32[10,4096]{1,0:T(8,128)S(1)} fusion(f32[512,10]{0,1:T(8,128)S(1)} %fusion.45, f32[4096,256]{1,0:T(8,128)S(1)} %copy-done, f32[4096,256]{1,0:T(8,128)S(1)} %copy-done.2), kind=kOutput, calls=%fused_computation.63 | convolution fusion | flops 253755392 | bytes 8572928 | tf_op jit(solution)/shard_map/dot_general | solution.py:45
  102.5 4.5 %fusion.47 = f32[512,10]{0,1:T(8,128)S(1)} fusion(f32[10,4096]{1,0:T(8,128)S(1)} %bitcast.235, f32[4096,256]{1,0:T(8,128)S(1)} %copy-done.14, f32[4096,256]{1,0:T(8,128)S(1)} %copy-done.12, f32[512]{0:T(512)S(1)} %get-tuple-element.109), kind=kOutput, calls=%fused_computation.75 | convolution fusion | flops 253760512 | bytes 8574976 | tf_op jit(solution)/shard_map/dot_general | solution.py:39
  107.0 7.2 %convolution_add_fusion.5 = f32[10,4096]{1,0:T(8,128)S(1)} fusion(f32[10,4096]{1,0:T(8,128)S(1)} %fusion.35, f32[512,10]{0,1:T(8,128)S(1)} %fusion.47, f32[4096,256]{1,0:T(8,128)S(1)} %copy-done.14, f32[4096,256]{1,0:T(8,128)S(1)} %copy-done.12), kind=kOutput, calls=%fused_computation.28 | convolution fusion | flops 253796352 | bytes 8736768 | tf_op jit(solution)/shard_map/dot_general | solution.py:45
  114.2 4.5 %fusion.49 = f32[512,10]{0,1:T(8,128)S(1)} fusion(f32[10,4096]{1,0:T(8,128)S(1)} %bitcast.236, f32[4096,256]{1,0:T(8,128)S(1)} %copy-done.10, f32[4096,256]{1,0:T(8,128)S(1)} %copy-done.8, f32[512]{0:T(512)S(1)} %get-tuple-element.110), kind=kOutput, calls=%fused_computation.77 | convolution fusion | flops 253760512 | bytes 8574976 | tf_op jit(solution)/shard_map/dot_general | solution.py:39
  118.7 7.4 %convolution_add_fusion.4 = f32[10,4096]{1,0:T(8,128)S(1)} fusion(f32[10,4096]{1,0:T(8,128)S(1)} %convolution_add_fusion.5, f32[512,10]{0,1:T(8,128)S(1)} %fusion.49, f32[4096,256]{1,0:T(8,128)S(1)} %copy-done.10, f32[4096,256]{1,0:T(8,128)S(1)} %copy-done.8), kind=kOutput, calls=%fused_computation.27 | convolution fusion | flops 253796352 | bytes 8736768 | tf_op jit(solution)/shard_map/dot_general | solution.py:45
  126.2 4.5 %fusion.51 = f32[512,10]{0,1:T(8,128)S(1)} fusion(f32[10,4096]{1,0:T(8,128)S(1)} %bitcast.237, f32[4096,256]{1,0:T(8,128)S(1)} %copy-done.6, f32[4096,256]{1,0:T(8,128)S(1)} %copy-done.4, f32[512]{0:T(512)S(1)} %get-tuple-element.111), kind=kOutput, calls=%fused_computation.79 | convolution fusion | flops 253760512 | bytes 8574976 | tf_op jit(solution)/shard_map/dot_general | solution.py:39
  130.6 7.2 %fusion.2 = bf16[10,1,4096]{2,0,1:T(8,128)(2,1)S(1)} fusion(f32[10,4096]{1,0:T(8,128)S(1)} %convolution_add_fusion.4, f32[512,10]{0,1:T(8,128)S(1)} %fusion.51, f32[4096,256]{1,0:T(8,128)S(1)} %copy-done.6, f32[4096,256]{1,0:T(8,128)S(1)} %copy-done.4), kind=kOutput, calls=%fused_computation.30 | convolution fusion | flops 253837312 | bytes 8654848 | tf_op jit(solution)/shard_map/dot_general | solution.py:45
  137.8 2.8 copy.22
  141.2 22.5 %reduce.8 = bf16[4096,10]{1,0:T(8,128)(2,1)S(1)} reduce(bf16[4096,1,10]{2,1,0:T(2,128)(2,1)S(1)} %bitcast.223, bf16[]{:T(256)} %broadcast.394), dimensions={1}, to_apply=%bitcast.201.reduce_sub_computation | reduce | bytes 163842
  163.6 2.5 reshape.231
  166.1 6.0 %all-to-all-start.1 = ((bf16[16,2,1280]{2,1,0:T(2,128)(2,1)}), bf16[16,2,1280]{2,1,0:T(2,128)(2,1)S(1)}, u32[]{:S(2)}, u32[]{:S(2)}) async-start(bf16[16,2,1280]{2,1,0:T(2,128)(2,1)} %reshape.231), calls=%async_computation.1 | async-start | bytes 163840 | tf_op jit(solution)/shard_map/all_to_all | solution.py:134
  172.2 7.0 %all-to-all-done.1 = bf16[16,2,1280]{2,1,0:T(2,128)(2,1)S(1)} async-done(((bf16[16,2,1280]{2,1,0:T(2,128)(2,1)}), bf16[16,2,1280]{2,1,0:T(2,128)(2,1)S(1)}, u32[]{:S(2)}, u32[]{:S(2)}) %all-to-all-start.1) | async-done | bytes 81952 | tf_op jit(solution)/shard_map/all_to_all | solution.py:134
  179.2 2.2 reshape.232
  181.5 2.1 copy.23
  184.4 7.6 %reduce-scatter.2.cloned.1.call-done = f32[3,8,256]{2,1,0:T(8,128)} async-done(((f32[3,16,256]{2,1,0:T(8,128)}), f32[3,8,256]{2,1,0:T(8,128)}) %reduce-scatter.2.cloned.1.call-update) | async-done | bytes 24592 | tf_op jit(solution)/shard_map/reduce_scatter | solution.py:140
  192.0 0.7 multiply_add_fusion.1
  193.0 1.8 collective-permute-start.1
  194.8 1.7 collective-permute-done
  196.8 4.4 %collective-permute-start.3 = (f32[3,16,4]{2,1,0:T(8,128)S(1)}, f32[3,16,4]{2,1,0:T(8,128)S(1)}, u32[]{:S(2)}, u32[]{:S(2)}) collective-permute-start(f32[3,16,4]{2,1,0:T(8,128)S(1)} %get-tuple-element.73), channel_id=1, source_target_pairs={{1,0},{2,1},{3,2},{4,3},{5,4},{6,5},{7,6},{8,7},{9,8},{10,9},{11,1... | collective-permute-start | bytes 2312 | tf_op jit(solution)/shard_map/ppermute | solution.py:21
  201.2 6.1 %gather_fusion.2 = f32[1024]{0:T(1024)S(1)} fusion(f32[2048]{0:T(1024)S(1)} %bitcast.221, s32[1024]{0:T(1024)S(1)} %get-tuple-element.36), kind=kCustom, calls=%fused_computation.2 | custom fusion | bytes 12288 | tf_op jit(solution)/shard_map/gather | solution.py:150
  208.4 6.2 %gather_fusion = f32[1024]{0:T(1024)S(1)} fusion(f32[2048]{0:T(1024)S(1)} %bitcast.222, s32[1024]{0:T(1024)S(1)} %get-tuple-element.36), kind=kCustom, calls=%fused_computation | custom fusion | bytes 12288 | tf_op jit(solution)/shard_map/gather | solution.py:150
  214.6 6.2 %gather_fusion.1 = f32[1024]{0:T(1024)S(1)} fusion(f32[2048]{0:T(1024)S(1)} %bitcast.220, s32[1024]{0:T(1024)S(1)} %get-tuple-element.36), kind=kCustom, calls=%fused_computation.1 | custom fusion | bytes 12288 | tf_op jit(solution)/shard_map/gather | solution.py:150
  220.8 6.0 %scatter_custom_fusion = f32[2048]{0:T(1024)S(1)} fusion(s32[1024]{0:T(1024)S(1)} %get-tuple-element.37, f32[1024]{0:T(1024)S(1)} %get-tuple-element.96, f32[]{:T(128)} %constant.175.clone.1), kind=kCustom, calls=%fused_computation.258 | custom fusion | flops 1024 | bytes 8196 | tf_op jit(solution)/shard_map/scatter-add | solution.py:157
  226.8 6.0 %scatter_custom_fusion.1 = f32[2048]{0:T(1024)S(1)} fusion(s32[1024]{0:T(1024)S(1)} %get-tuple-element.37, f32[1024]{0:T(1024)S(1)} %get-tuple-element.97, f32[]{:T(128)} %constant.175.clone.1), kind=kCustom, calls=%fused_computation.256 | custom fusion | flops 1024 | bytes 8196 | tf_op jit(solution)/shard_map/scatter-add | solution.py:157
  232.8 2.0 collective-permute-start.4
  234.9 1.7 collective-permute-done.4
  236.6 1.9 collective-permute-done.5
  238.6 4.4 %collective-permute-start.7 = (f32[4,16,4]{2,1,0:T(8,128)S(1)}, f32[4,16,4]{2,1,0:T(8,128)S(1)}, u32[]{:S(2)}, u32[]{:S(2)}) collective-permute-start(f32[4,16,4]{2,1,0:T(8,128)S(1)} %get-tuple-element.71), channel_id=1, source_target_pairs={{1,0},{2,1},{3,2},{4,3},{5,4},{6,5},{7,6},{8,7},{9,8},{10,9},{11,1... | collective-permute-start | bytes 3080 | tf_op jit(solution)/shard_map/ppermute | solution.py:21
  243.1 6.0 %scatter_custom_fusion.2 = f32[2048]{0:T(1024)S(1)} fusion(s32[1024]{0:T(1024)S(1)} %get-tuple-element.37, f32[1024]{0:T(1024)S(1)} %get-tuple-element.32, f32[]{:T(128)} %constant.175.clone.1), kind=kCustom, calls=%fused_computation.254 | custom fusion | flops 1024 | bytes 8196 | tf_op jit(solution)/shard_map/scatter-add | solution.py:157
  250.7 4.4 %all_gather.3 = bf16[3,16,256]{2,1,0:T(8,128)(2,1)S(1)} all-gather(bf16[3,8,256]{2,1,0:T(8,128)(2,1)S(1)} %get-tuple-element.77), channel_id=1, replica_groups=mesh['grp'=2,'sp'=16] {'grp'}, dimensions={1}, use_global_device_ids=true | all-gather | bytes 36864 | tf_op jit(solution)/shard_map/all_gather | solution.py:177
  255.2 12.6 %all_to_all.35 = f32[10,16,256]{2,0,1:T(8,128)S(1)} all-to-all(f32[10,16,256]{2,0,1:T(8,128)S(1)} %bitcast.231), channel_id=1, replica_groups=mesh['grp'=2,'sp'=16] {'sp'}, dimensions={1} | all-to-all | bytes 327680 | tf_op jit(solution)/shard_map/all_to_all | solution.py:131
  268.2 4.9 %fusion.52 = f32[10,512]{1,0:T(8,128)S(1)} fusion(f32[10,4096]{1,0:T(8,128)S(1)} %bitcast.225, f32[4096,256]{1,0:T(8,128)} %get-tuple-element.103, f32[4096,256]{1,0:T(8,128)S(1)} %copy-done.5, f32[512]{0:T(512)S(1)} %get-tuple-element.111), kind=kOutput, calls=%fused_computation.80 | convolution fusion | flops 253760512 | bytes 8574976 | tf_op jit(solution)/shard_map/dot_general | solution.py:39
  273.1 4.1 %fusion.50 = f32[10,512]{1,0:T(8,128)S(1)} fusion(f32[10,4096]{1,0:T(8,128)S(1)} %bitcast.226, f32[4096,256]{1,0:T(8,128)S(1)} %copy-done.11, f32[4096,256]{1,0:T(8,128)S(1)} %copy-done.9, f32[512]{0:T(512)S(1)} %get-tuple-element.110), kind=kOutput, calls=%fused_computation.78 | convolution fusion | flops 253760512 | bytes 8574976 | tf_op jit(solution)/shard_map/dot_general | solution.py:39
  277.2 4.1 %fusion.48 = f32[10,512]{1,0:T(8,128)S(1)} fusion(f32[10,4096]{1,0:T(8,128)S(1)} %bitcast.227, f32[4096,256]{1,0:T(8,128)S(1)} %copy-done.15, f32[4096,256]{1,0:T(8,128)S(1)} %copy-done.13, f32[512]{0:T(512)S(1)} %get-tuple-element.109), kind=kOutput, calls=%fused_computation.76 | convolution fusion | flops 253760512 | bytes 8574976 | tf_op jit(solution)/shard_map/dot_general | solution.py:39
  281.3 4.3 %fusion.46 = f32[10,512]{1,0:T(8,128)S(1)} fusion(f32[10,4096]{1,0:T(8,128)S(1)} %bitcast.228, f32[4096,256]{1,0:T(8,128)S(1)} %copy-done.1, f32[4096,256]{1,0:T(8,128)S(1)} %copy-done.3, f32[512]{0:T(512)S(1)} %get-tuple-element.108), kind=kOutput, calls=%fused_computation.74 | convolution fusion | flops 253760512 | bytes 8574976 | tf_op jit(solution)/shard_map/dot_general | solution.py:39
  285.5 7.0 %fusion.33 = f32[10,4096]{1,0:T(8,128)S(1)} fusion(f32[10,512]{1,0:T(8,128)S(1)} %fusion.46, f32[4096,256]{1,0:T(8,128)S(1)} %copy-done.1, f32[4096,256]{1,0:T(8,128)S(1)} %copy-done.3), kind=kOutput, calls=%fused_computation.61 | convolution fusion | flops 253755392 | bytes 8572928 | tf_op jit(solution)/shard_map/dot_general | solution.py:45
  292.5 7.2 %convolution_add_fusion.2 = f32[10,4096]{1,0:T(8,128)S(1)} fusion(f32[10,4096]{1,0:T(8,128)S(1)} %fusion.33, f32[10,512]{1,0:T(8,128)S(1)} %fusion.48, f32[4096,256]{1,0:T(8,128)S(1)} %copy-done.15, f32[4096,256]{1,0:T(8,128)S(1)} %copy-done.13), kind=kOutput, calls=%fused_computation.25 | convolution fusion | flops 253796352 | bytes 8736768 | tf_op jit(solution)/shard_map/dot_general | solution.py:45
  299.7 7.0 %convolution_add_fusion.1 = f32[10,4096]{1,0:T(8,128)S(1)} fusion(f32[10,4096]{1,0:T(8,128)S(1)} %convolution_add_fusion.2, f32[10,512]{1,0:T(8,128)S(1)} %fusion.50, f32[4096,256]{1,0:T(8,128)S(1)} %copy-done.11, f32[4096,256]{1,0:T(8,128)S(1)} %copy-done.9), kind=kOutput, calls=%fused_computation.24 | convolution fusion | flops 253796352 | bytes 8736768 | tf_op jit(solution)/shard_map/dot_general | solution.py:45
  306.8 7.0 %fusion = f32[10,1,4096]{2,0,1:T(8,128)S(1)} fusion(f32[10,4096]{1,0:T(8,128)S(1)} %convolution_add_fusion.1, f32[10,512]{1,0:T(8,128)S(1)} %fusion.52, f32[4096,256]{1,0:T(8,128)S(1)} %copy-done.7, f32[4096,256]{1,0:T(8,128)S(1)} %copy-done.5), kind=kOutput, calls=%fused_computation.23 | convolution fusion | flops 253796352 | bytes 8736768 | tf_op jit(solution)/shard_map/dot_general | solution.py:45
  314.1 11.1 %all_to_all.36 = f32[16,10,1,256]{3,2,1,0:T(1,128)S(1)} all-to-all(f32[16,10,1,256]{3,2,1,0:T(1,128)S(1)} %copy.25), channel_id=1, replica_groups=mesh['grp'=2,'sp'=16] {'sp'}, dimensions={0} | all-to-all | bytes 327680 | tf_op jit(solution)/shard_map/all_to_all | solution.py:182
  325.3 0.7 bitcast_add_fusion
  (152 shorter events, 5.8 us)
Async XLA Ops:
  8.9 78.7 %all-to-all-start = ((f32[10,16,256]{2,0,1:T(8,128)}), f32[10,16,256]{2,0,1:T(8,128)S(1)}, u32[]{:S(2)}, u32[]{:S(2)}) async-start(f32[10,16,256]{2,0,1:T(8,128)} %copy.20), calls=%async_computation | async-start | bytes 524288 | tf_op jit(solution)/shard_map/all_to_all | solution.py:131
  16.3 17.7 %copy-start.23 = (f32[1024]{0:T(1024)S(1)}, f32[1024]{0:T(1024)}, u32[]{:S(2)}) copy-start(f32[1024]{0:T(1024)} %param.17) | copy-start | bytes 12292
  69.7 17.9 %copy-start.24 = (s32[1024]{0:T(1024)S(1)}, s32[1024]{0:T(1024)}, u32[]{:S(2)}) copy-start(s32[1024]{0:T(1024)} %param.18) | copy-start | bytes 12292
  87.9 7.5 %copy-start = (f32[4096,256]{1,0:T(8,128)S(1)}, f32[4096,256]{1,0:T(8,128)}, u32[]{:S(2)}) copy-start(f32[4096,256]{1,0:T(8,128)} %get-tuple-element.112) | copy-start | bytes 12582916
  87.9 7.5 %copy-start.2 = (f32[4096,256]{1,0:T(8,128)S(1)}, f32[4096,256]{1,0:T(8,128)}, u32[]{:S(2)}) copy-start(f32[4096,256]{1,0:T(8,128)} %get-tuple-element.113) | copy-start | bytes 12582916
  95.5 7.0 %copy-start.12 = (f32[4096,256]{1,0:T(8,128)S(1)}, f32[4096,256]{1,0:T(8,128)}, u32[]{:S(2)}) copy-start(f32[4096,256]{1,0:T(8,128)} %get-tuple-element.106) | copy-start | bytes 12582916
  95.5 7.0 %copy-start.14 = (f32[4096,256]{1,0:T(8,128)S(1)}, f32[4096,256]{1,0:T(8,128)}, u32[]{:S(2)}) copy-start(f32[4096,256]{1,0:T(8,128)} %get-tuple-element.107) | copy-start | bytes 12582916
  107.0 7.2 %copy-start.8 = (f32[4096,256]{1,0:T(8,128)S(1)}, f32[4096,256]{1,0:T(8,128)}, u32[]{:S(2)}) copy-start(f32[4096,256]{1,0:T(8,128)} %get-tuple-element.104) | copy-start | bytes 12582916
  107.0 7.2 %copy-start.10 = (f32[4096,256]{1,0:T(8,128)S(1)}, f32[4096,256]{1,0:T(8,128)}, u32[]{:S(2)}) copy-start(f32[4096,256]{1,0:T(8,128)} %get-tuple-element.105) | copy-start | bytes 12582916
  118.7 7.4 %copy-start.4 = (f32[4096,256]{1,0:T(8,128)S(1)}, f32[4096,256]{1,0:T(8,128)}, u32[]{:S(2)}) copy-start(f32[4096,256]{1,0:T(8,128)} %get-tuple-element.102) | copy-start | bytes 12582916
  118.7 7.4 %copy-start.6 = (f32[4096,256]{1,0:T(8,128)S(1)}, f32[4096,256]{1,0:T(8,128)}, u32[]{:S(2)}) copy-start(f32[4096,256]{1,0:T(8,128)} %get-tuple-element.103) | copy-start | bytes 12582916
  141.1 42.5 %copy-start.16 = (bf16[10,3,16,256]{3,2,1,0:T(8,128)(2,1)S(1)}, bf16[10,3,16,256]{3,2,1,0:T(8,128)(2,1)}, u32[]{:S(2)}) copy-start(bf16[10,3,16,256]{3,2,1,0:T(8,128)(2,1)} %param.14) | copy-start | bytes 737284
  141.2 50.8 %copy-start.18 = (f32[3,8,256]{2,1,0:T(8,128)S(1)}, f32[3,8,256]{2,1,0:T(8,128)}, u32[]{:S(2)}) copy-start(f32[3,8,256]{2,1,0:T(8,128)} %param.16) | copy-start | bytes 73732
  141.2 50.8 %copy-start.19 = (f32[3,8,256]{2,1,0:T(8,128)S(1)}, f32[3,8,256]{2,1,0:T(8,128)}, u32[]{:S(2)}) copy-start(f32[3,8,256]{2,1,0:T(8,128)} %param.15) | copy-start | bytes 73732
  166.1 13.1 %all-to-all-start.1 = ((bf16[16,2,1280]{2,1,0:T(2,128)(2,1)}), bf16[16,2,1280]{2,1,0:T(2,128)(2,1)S(1)}, u32[]{:S(2)}, u32[]{:S(2)}) async-start(bf16[16,2,1280]{2,1,0:T(2,128)(2,1)} %reshape.231), calls=%async_computation.1 | async-start | bytes 163840 | tf_op jit(solution)/shard_map/all_to_all | solution.py:134
  172.1 19.9 %reduce-scatter.2.cloned.1.call-start = ((), (), s32[]{:S(2)}) async-start(), calls=%async_computation.5 | async-start | bytes 73728 | tf_op jit(solution)/shard_map/reduce_scatter | solution.py:140
  192.7 3.8 %collective-permute-start = (f32[3,4,256]{2,1,0:T(4,128)S(1)}, f32[3,4,256]{2,1,0:T(4,128)S(1)}, u32[]{:S(2)}, u32[]{:S(2)}) collective-permute-start(f32[3,4,256]{2,1,0:T(4,128)S(1)} %get-tuple-element.94), channel_id=1, source_target_pairs={{0,16},{16,0},{1,17},{17,1},{2,18},{18,2},{3,19},{19,3},{4,20},{20... | collective-permute-start | bytes 36872 | tf_op jit(solution)/shard_map/ppermute | solution.py:18
  193.0 3.7 %collective-permute-start.1 = (f32[3,4,256]{2,1,0:T(4,128)S(1)}, f32[3,4,256]{2,1,0:T(4,128)S(1)}, u32[]{:S(2)}, u32[]{:S(2)}) collective-permute-start(f32[3,4,256]{2,1,0:T(4,128)S(1)} %get-tuple-element.95), channel_id=1, source_target_pairs={{16,0},{0,16},{17,1},{1,17},{18,2},{2,18},{19,3},{3,19},{20,4},{4,... | collective-permute-start | bytes 36872 | tf_op jit(solution)/shard_map/ppermute | solution.py:21
  196.8 10.6 %collective-permute-start.2 = (f32[3,16,4]{2,1,0:T(8,128)S(1)}, f32[3,16,4]{2,1,0:T(8,128)S(1)}, u32[]{:S(2)}, u32[]{:S(2)}) collective-permute-start(f32[3,16,4]{2,1,0:T(8,128)S(1)} %get-tuple-element.72), channel_id=1, source_target_pairs={{0,1},{1,2},{2,3},{3,4},{4,5},{5,6},{6,7},{7,8},{8,9},{9,10},{10,1... | collective-permute-start | bytes 2312 | tf_op jit(solution)/shard_map/ppermute | solution.py:18
  196.8 10.6 %collective-permute-start.3 = (f32[3,16,4]{2,1,0:T(8,128)S(1)}, f32[3,16,4]{2,1,0:T(8,128)S(1)}, u32[]{:S(2)}, u32[]{:S(2)}) collective-permute-start(f32[3,16,4]{2,1,0:T(8,128)S(1)} %get-tuple-element.73), channel_id=1, source_target_pairs={{1,0},{2,1},{3,2},{4,3},{5,4},{6,5},{7,6},{8,7},{9,8},{10,9},{11,1... | collective-permute-start | bytes 2312 | tf_op jit(solution)/shard_map/ppermute | solution.py:21
  208.4 12.4 %copy-start.20 = (f32[1024]{0:T(1024)S(1)}, f32[1024]{0:T(1024)}, u32[]{:S(2)}) copy-start(f32[1024]{0:T(1024)} %param.21) | copy-start | bytes 12292
  208.4 12.4 %copy-start.21 = (f32[1024]{0:T(1024)S(1)}, f32[1024]{0:T(1024)}, u32[]{:S(2)}) copy-start(f32[1024]{0:T(1024)} %param.20) | copy-start | bytes 12292
  208.4 12.4 %copy-start.22 = (s32[1024]{0:T(1024)S(1)}, s32[1024]{0:T(1024)}, u32[]{:S(2)}) copy-start(s32[1024]{0:T(1024)} %param.19) | copy-start | bytes 12292
  232.8 3.8 %collective-permute-start.4 = (f32[4,4,256]{2,1,0:T(4,128)S(1)}, f32[4,4,256]{2,1,0:T(4,128)S(1)}, u32[]{:S(2)}, u32[]{:S(2)}) collective-permute-start(f32[4,4,256]{2,1,0:T(4,128)S(1)} %get-tuple-element.74), channel_id=1, source_target_pairs={{0,16},{16,0},{1,17},{17,1},{2,18},{18,2},{3,19},{19,3},{4,20},{20... | collective-permute-start | bytes 49160 | tf_op jit(solution)/shard_map/ppermute | solution.py:18
  234.8 3.7 %collective-permute-start.5 = (f32[4,4,256]{2,1,0:T(4,128)S(1)}, f32[4,4,256]{2,1,0:T(4,128)S(1)}, u32[]{:S(2)}, u32[]{:S(2)}) collective-permute-start(f32[4,4,256]{2,1,0:T(4,128)S(1)} %get-tuple-element.75), channel_id=1, source_target_pairs={{16,0},{0,16},{17,1},{1,17},{18,2},{2,18},{19,3},{3,19},{20,4},{4,... | collective-permute-start | bytes 49160 | tf_op jit(solution)/shard_map/ppermute | solution.py:21
  238.6 10.4 %collective-permute-start.6 = (f32[4,16,4]{2,1,0:T(8,128)S(1)}, f32[4,16,4]{2,1,0:T(8,128)S(1)}, u32[]{:S(2)}, u32[]{:S(2)}) collective-permute-start(f32[4,16,4]{2,1,0:T(8,128)S(1)} %get-tuple-element.70), channel_id=1, source_target_pairs={{0,1},{1,2},{2,3},{3,4},{4,5},{5,6},{6,7},{7,8},{8,9},{9,10},{10,1... | collective-permute-start | bytes 3080 | tf_op jit(solution)/shard_map/ppermute | solution.py:18
  238.6 10.4 %collective-permute-start.7 = (f32[4,16,4]{2,1,0:T(8,128)S(1)}, f32[4,16,4]{2,1,0:T(8,128)S(1)}, u32[]{:S(2)}, u32[]{:S(2)}) collective-permute-start(f32[4,16,4]{2,1,0:T(8,128)S(1)} %get-tuple-element.71), channel_id=1, source_target_pairs={{1,0},{2,1},{3,2},{4,3},{5,4},{6,5},{7,6},{8,7},{9,8},{10,9},{11,1... | collective-permute-start | bytes 3080 | tf_op jit(solution)/shard_map/ppermute | solution.py:21
  249.0 19.1 %copy-start.5 = (f32[4096,256]{1,0:T(8,128)S(1)}, f32[4096,256]{1,0:T(8,128)}, u32[]{:S(2)}) copy-start(f32[4096,256]{1,0:T(8,128)} %get-tuple-element.102) | copy-start | bytes 12582916
  268.1 4.9 %copy-start.9 = (f32[4096,256]{1,0:T(8,128)S(1)}, f32[4096,256]{1,0:T(8,128)}, u32[]{:S(2)}) copy-start(f32[4096,256]{1,0:T(8,128)} %get-tuple-element.104) | copy-start | bytes 12582916
  268.1 4.9 %copy-start.11 = (f32[4096,256]{1,0:T(8,128)S(1)}, f32[4096,256]{1,0:T(8,128)}, u32[]{:S(2)}) copy-start(f32[4096,256]{1,0:T(8,128)} %get-tuple-element.105) | copy-start | bytes 12582916
  273.1 4.1 %copy-start.13 = (f32[4096,256]{1,0:T(8,128)S(1)}, f32[4096,256]{1,0:T(8,128)}, u32[]{:S(2)}) copy-start(f32[4096,256]{1,0:T(8,128)} %get-tuple-element.106) | copy-start | bytes 12582916
  273.1 4.1 %copy-start.15 = (f32[4096,256]{1,0:T(8,128)S(1)}, f32[4096,256]{1,0:T(8,128)}, u32[]{:S(2)}) copy-start(f32[4096,256]{1,0:T(8,128)} %get-tuple-element.107) | copy-start | bytes 12582916
  277.2 4.1 %copy-start.1 = (f32[4096,256]{1,0:T(8,128)S(1)}, f32[4096,256]{1,0:T(8,128)}, u32[]{:S(2)}) copy-start(f32[4096,256]{1,0:T(8,128)} %get-tuple-element.112) | copy-start | bytes 12582916
  277.2 4.1 %copy-start.3 = (f32[4096,256]{1,0:T(8,128)S(1)}, f32[4096,256]{1,0:T(8,128)}, u32[]{:S(2)}) copy-start(f32[4096,256]{1,0:T(8,128)} %get-tuple-element.113) | copy-start | bytes 12582916
  299.7 7.0 %copy-start.7 = (f32[4096,256]{1,0:T(8,128)S(1)}, f32[4096,256]{1,0:T(8,128)}, u32[]{:S(2)}) copy-start(f32[4096,256]{1,0:T(8,128)} %get-tuple-element.103) | copy-start | bytes 12582916
  306.8 18.5 %copy-start.17 = (f32[10,16,256]{2,1,0:T(8,128)S(1)}, f32[10,16,256]{2,1,0:T(8,128)}, u32[]{:S(2)}) copy-start(f32[10,16,256]{2,1,0:T(8,128)} %param.13) | copy-start | bytes 491524
Sparse Core Ops, SparseCore 0:
  184.5 7.4 reduce-scatter.1
